TPU v7x, 32 devices: a whole 2x2x4 slice. The times are simulated.
32 devices in a mesh: dep: 4 (over z), col: 2 (over y), row: 4 (over x, core).
Axes of the slice: x: 2, y: 2, z: 4, core: 2. Of those that a mesh axis runs over, the one named last changes fastest.
Arguments:
- tokens: bfloat16 [32768, 1280], P(('dep', 'row'), 'col')
- w_up1: bfloat16 [1280, 5120], P('row', 'col')
- w_down1: bfloat16 [5120, 1280], P('row', 'col')
- w_up2: bfloat16 [1280, 5120], P('row', 'col')
- w_down2: bfloat16 [5120, 1280], P('row', 'col')
- grad_out: bfloat16 [32768, 1280], P(('dep', 'row'), 'col')
Outputs:
- output 1: bfloat16 [32768, 1280], P(('dep', 'row'), 'col')
- output 2: bfloat16 [32768, 1280], P(('dep', 'row'), 'col')
- output 3: float32 [1280, 5120], P('row', 'col')
- output 4: float32 [5120, 1280], P('row', 'col')
- output 5: float32 [1280, 5120], P('row', 'col')
- output 6: float32 [5120, 1280], P('row', 'col')
All inputs are finite; a program needn't handle non-finite values.
Results may differ from a plain program's by a relative error of at most 0.00457.
Values are sent between devices in bfloat16 or wider.
A program may use at most 1 GiB of HBM per device.

v0:
```python
import jax
import jax.numpy as jnp
from jax import lax
from jax.sharding import PartitionSpec as P


def gelu_tanh(pre_act):
    return jax.nn.gelu(pre_act, approximate=True)


def gelu_grad(pre_act, grad_hidden):
    return jax.vjp(gelu_tanh, pre_act)[1](grad_hidden)[0]


def dot_last(left_op, right_op):
    return lax.dot_general(left_op, right_op, (((1,), (1,)), ((), ())), preferred_element_type=jnp.float32)


def dot_first(left_op, right_op):
    return lax.dot_general(left_op, right_op, (((0,), (0,)), ((), ())), preferred_element_type=jnp.float32)


def block_forward(block_in, w_up, w_down):
    acts_full = lax.all_gather(block_in, "col", axis=1, tiled=True)
    up_cols = lax.all_gather(w_up, "row", axis=0, tiled=True)
    pre_act = jnp.dot(acts_full, up_cols, preferred_element_type=jnp.float32)
    hidden = gelu_tanh(pre_act).astype(jnp.bfloat16)
    hidden_full = lax.all_gather(hidden, "col", axis=1, tiled=True)
    down_cols = lax.all_gather(w_down, "row", axis=0, tiled=True)
    mlp_out = jnp.dot(hidden_full, down_cols, preferred_element_type=jnp.float32)
    result = (block_in.astype(jnp.float32) + mlp_out).astype(jnp.bfloat16)
    return result, (acts_full, up_cols, pre_act, hidden_full, down_cols)


def block_backward(saved_acts, grad_res):
    acts_full, up_cols, pre_act, hidden_full, down_cols = saved_acts
    hidden_part = dot_last(grad_res, down_cols)
    grad_hidden = lax.psum_scatter(hidden_part, "col", scatter_dimension=1, tiled=True)
    grad_pre = gelu_grad(pre_act, grad_hidden).astype(jnp.bfloat16)
    input_part = dot_last(grad_pre, up_cols)
    input_sum = lax.psum_scatter(input_part, "col", scatter_dimension=1, tiled=True)
    grad_in = (grad_res.astype(jnp.float32) + input_sum).astype(jnp.bfloat16)
    down_part = dot_first(hidden_full, grad_res)
    grad_down = lax.psum(lax.psum_scatter(down_part, "row", scatter_dimension=0, tiled=True), "dep")
    up_part = dot_first(acts_full, grad_pre)
    grad_up = lax.psum(lax.psum_scatter(up_part, "row", scatter_dimension=0, tiled=True), "dep")
    return grad_in, grad_up, grad_down


def solution(mesh):
    act_spec = P(("dep", "row"), "col")
    weight_spec = P("row", "col")

    def local_step(tokens, w_up1, w_down1, w_up2, w_down2, grad_out):
        mid_acts, saved_first = block_forward(tokens, w_up1, w_down1)
        y_out, saved_second = block_forward(mid_acts, w_up2, w_down2)
        grad_mid, grad_up2, grad_down2 = block_backward(saved_second, grad_out)
        grad_x, grad_up1, grad_down1 = block_backward(saved_first, grad_mid)
        return y_out, grad_x, grad_up1, grad_down1, grad_up2, grad_down2

    return jax.shard_map(local_step, mesh=mesh, in_specs=(act_spec, weight_spec, weight_spec, weight_spec, weight_spec, act_spec), out_specs=(act_spec, act_spec, weight_spec, weight_spec, weight_spec, weight_spec), check_vma=False)
```

profile of v0, /device:TPU:0, one launch (start us, length us, event | category | flops | bytes accessed | tf_op | source)
XLA Modules:
  0.0 2989.2 jit_solution(549607202568702100)
XLA Ops:
  9.4 71.9 %all-gather.9.cloned.1.call-done = bf16[2048,1280]{1,0:T(8,128)(2,1)} async-done(((bf16[2048,640]{1,0:T(8,128)(2,1)}), bf16[2048,1280]{1,0:T(8,128)(2,1)}) %all-gather.9.cloned.1.call-update) | async-done | bytes 5242896 | tf_op jit(solution)/shard_map/all_gather | solution.py:24
  81.3 49.5 %all-gather.11.cloned.1.call-done = bf16[1280,2560]{1,0:T(8,128)(2,1)} async-done(((bf16[320,2560]{1,0:T(8,128)(2,1)}), bf16[1280,2560]{1,0:T(8,128)(2,1)}) %all-gather.11.cloned.1.call-update) | async-done | bytes 6553616 | tf_op jit(solution)/shard_map/all_gather | solution.py:25
  130.8 26.7 multiply_convert_fusion.1
  159.0 21.3 all-gather.15.cloned.1.call-done
  180.3 249.2 %all-gather.13.cloned.1.call-done = bf16[2048,5120]{1,0:T(8,128)(2,1)} async-done(((bf16[2048,2560]{1,0:T(8,128)(2,1)}), bf16[2048,5120]{1,0:T(8,128)(2,1)}) %all-gather.13.cloned.1.call-update) | async-done | bytes 20971536 | tf_op jit(solution)/shard_map/all_gather | solution.py:28
  429.5 22.5 add_convert_fusion.3
  452.0 26.8 all-gather.23.cloned.1.call-done
  478.8 23.8 fusion.14
  503.1 25.0 all-gather.19.cloned.1.call-done
  528.2 71.1 %all-gather.17.cloned.1.call-done = bf16[2048,1280]{1,0:T(8,128)(2,1)} async-done(((bf16[2048,640]{1,0:T(8,128)(2,1)}), bf16[2048,1280]{1,0:T(8,128)(2,1)}) %all-gather.17.cloned.1.call-update) | async-done | bytes 5242896 | tf_op jit(solution)/shard_map/all_gather | solution.py:24
  599.3 461.2 %reduce-scatter.11.cloned.1.call-done = f32[2048,2560]{1,0:T(8,128)} async-done(((f32[2048,5120]{1,0:T(8,128)}), f32[2048,2560]{1,0:T(8,128)}) %reduce-scatter.11.cloned.1.call-update) | async-done | bytes 20971536 | tf_op jit(solution)/shard_map/reduce_scatter | solution.py:38
  1060.5 34.7 %fusion.13 = (bf16[2048,2560]{1,0:T(8,128)(2,1)}, bf16[2048,2560]{1,0:T(8,128)(2,1)}) fusion(f32[2048,2560]{1,0:T(8,128)} %reduce-scatter.11.cloned.1.call-done, bf16[2048,1280]{1,0:T(8,128)(2,1)} %all-gather.17.cloned.1.call-done, bf16[1280,2560]{1,0:T(8,128)(2,1)} %all-gather.19.cloned.1.call-done), kind=kOutput, calls=%fused_computation.17 | convolution fusion | flops 13537116160 | bytes 53739520 | tf_op jit(solution)/shard_map/dot_general | solution.py:26
  1095.2 17.7 fusion.15
  1112.9 121.9 %reduce-scatter.13.cloned.1.call-done = f32[2048,640]{1,0:T(8,128)} async-done(((f32[2048,1280]{1,0:T(8,128)}), f32[2048,640]{1,0:T(8,128)}) %reduce-scatter.13.cloned.1.call-update) | async-done | bytes 5242896 | tf_op jit(solution)/shard_map/reduce_scatter | solution.py:41
  1238.7 23.9 fusion.16
  1263.5 458.1 %reduce-scatter.15.cloned.1.call-done = f32[2048,2560]{1,0:T(8,128)} async-done(((f32[2048,5120]{1,0:T(8,128)}), f32[2048,2560]{1,0:T(8,128)}) %reduce-scatter.15.cloned.1.call-update) | async-done | bytes 20971536 | tf_op jit(solution)/shard_map/reduce_scatter | solution.py:38
  1721.6 18.8 fusion.6
  1744.3 19.5 convolution_bitcast_fusion
  1763.8 14.0 copy.14
  1778.1 20.9 fusion.19
  1799.1 171.8 %all-gather.21.cloned.1.call-done = bf16[2048,5120]{1,0:T(8,128)(2,1)} async-done(((bf16[2048,2560]{1,0:T(8,128)(2,1)}), bf16[2048,5120]{1,0:T(8,128)(2,1)}) %all-gather.21.cloned.1.call-update) | async-done | bytes 20971536 | tf_op jit(solution)/shard_map/all_gather | solution.py:28
  1970.9 22.2 fusion.20
  1993.5 21.6 fusion.18
  2015.1 19.5 fusion.17
  2034.7 38.0 %reduce-scatter.25.cloned.1.call-done = f32[320,2560]{1,0:T(8,128)} async-done(((f32[1280,2560]{1,0:T(8,128)}), f32[320,2560]{1,0:T(8,128)}) %reduce-scatter.25.cloned.1.call-update) | async-done | bytes 3276816
  2077.8 96.8 %reduce-scatter.21.cloned.1.call-done = f32[320,2560]{1,0:T(8,128)} async-done(((f32[1280,2560]{1,0:T(8,128)}), f32[320,2560]{1,0:T(8,128)}) %reduce-scatter.21.cloned.1.call-update) | async-done | bytes 3276816 | tf_op jit(solution)/shard_map/reduce_scatter | solution.py:46
  2174.7 101.8 %reduce-scatter.23.cloned.1.call-done = f32[1280,640]{1,0:T(8,128)} async-done(((f32[5120,640]{1,0:T(8,128)}), f32[1280,640]{1,0:T(8,128)}) %reduce-scatter.23.cloned.1.call-update) | async-done | bytes 3276816 | tf_op jit(solution)/shard_map/reduce_scatter | solution.py:44
  2276.5 101.8 %reduce-scatter.19.cloned.1.call-done = f32[1280,640]{1,0:T(8,128)} async-done(((f32[5120,640]{1,0:T(8,128)}), f32[1280,640]{1,0:T(8,128)}) %reduce-scatter.19.cloned.1.call-update) | async-done | bytes 3276816 | tf_op jit(solution)/shard_map/reduce_scatter | solution.py:44
  2378.3 22.5 add_convert_fusion.2
  2400.7 101.5 %reduce-scatter.17.cloned.1.call-done = f32[2048,640]{1,0:T(8,128)} async-done(((f32[2048,1280]{1,0:T(8,128)}), f32[2048,640]{1,0:T(8,128)}) %reduce-scatter.17.cloned.1.call-update) | async-done | bytes 5242896 | tf_op jit(solution)/shard_map/reduce_scatter | solution.py:41
  2506.8 460.7 %all-reduce.3.cloned.1.call-done = (f32[320,2560]{0,1:T(8,128)}, f32[1280,640]{1,0:T(8,128)}, f32[320,2560]{1,0:T(8,128)}, f32[1280,640]{1,0:T(8,128)}) async-done(((f32[320,2560]{0,1:T(8,128)}, f32[1280,640]{1,0:T(8,128)}, f32[320,2560]{1,0:T(8,128)}, f32[1280,640]{1,0:T(8,128)}), (f32[320,2560]{0,1:T(8,128)}, f32[1280,640]{1,0:T(8,128)}, f32[320,2560]{1,0:T(8,128)}, ...) | async-done | bytes 13107216 | tf_op jit(solution)/shard_map/psum | solution.py:46
  2967.4 5.4 copy.13
  (48 shorter events, 32.6 us)
Async XLA Ops:
  7.2 74.1 %all-gather.9.cloned.1.call-start = ((), (), s32[]{:S(2)}) async-start(), calls=%async_computation.8 | async-start | bytes 7864320 | tf_op jit(solution)/shard_map/all_gather | solution.py:24
  7.9 122.9 %all-gather.11.cloned.1.call-start = ((), (), s32[]{:S(2)}) async-start(), calls=%async_computation.9 | async-start | bytes 8192000 | tf_op jit(solution)/shard_map/all_gather | solution.py:25
  8.6 171.6 %all-gather.15.cloned.1.call-start = ((), (), s32[]{:S(2)}) async-start(), calls=%async_computation.11 | async-start | bytes 8192000 | tf_op jit(solution)/shard_map/all_gather | solution.py:29
  9.4 420.1 %all-gather.13.cloned.1.call-start = ((), (), s32[]{:S(2)}) async-start(), calls=%async_computation.10 | async-start | bytes 31457280 | tf_op jit(solution)/shard_map/all_gather | solution.py:28
  157.5 321.3 %all-gather.23.cloned.1.call-start = ((), (), s32[]{:S(2)}) async-start(), calls=%async_computation.15 | async-start | bytes 8192000 | tf_op jit(solution)/shard_map/all_gather | solution.py:29
  158.1 370.0 %all-gather.19.cloned.1.call-start = ((), (), s32[]{:S(2)}) async-start(), calls=%async_computation.13 | async-start | bytes 8192000 | tf_op jit(solution)/shard_map/all_gather | solution.py:25
  158.7 320.1 %copy-start.2 = (bf16[2048,640]{1,0:T(8,128)(2,1)S(1)}, bf16[2048,640]{1,0:T(8,128)(2,1)}, u32[]{:S(2)}) copy-start(bf16[2048,640]{1,0:T(8,128)(2,1)} %param.11) | copy-start | bytes 7864324
  158.7 440.6 %all-gather.17.cloned.1.call-start = ((), (), s32[]{:S(2)}) async-start(), calls=%async_computation.12 | async-start | bytes 7864320 | tf_op jit(solution)/shard_map/all_gather | solution.py:24
  451.9 608.6 %reduce-scatter.11.cloned.1.call-start = ((), (), s32[]{:S(2)}) async-start(), calls=%async_computation.16 | async-start | bytes 62914560 | tf_op jit(solution)/shard_map/reduce_scatter | solution.py:38
  502.7 732.2 %reduce-scatter.13.cloned.1.call-start = ((), (), s32[]{:S(2)}) async-start(), calls=%async_computation.17 | async-start | bytes 15728640 | tf_op jit(solution)/shard_map/reduce_scatter | solution.py:41
  1060.5 34.7 %copy-start.3 = (bf16[1280,2560]{1,0:T(8,128)(2,1)S(1)}, bf16[1280,2560]{1,0:T(8,128)(2,1)}, u32[]{:S(2)}) copy-start(bf16[1280,2560]{1,0:T(8,128)(2,1)} %all-gather.19.cloned.1.call-done) | copy-start | bytes 19660804
  1112.9 608.7 %reduce-scatter.15.cloned.1.call-start = ((), (), s32[]{:S(2)}) async-start(), calls=%async_computation.18 | async-start | bytes 62914560 | tf_op jit(solution)/shard_map/reduce_scatter | solution.py:38
  1262.6 708.4 %all-gather.21.cloned.1.call-start = ((), (), s32[]{:S(2)}) async-start(), calls=%async_computation.14 | async-start | bytes 31457280 | tf_op jit(solution)/shard_map/all_gather | solution.py:28
  1263.3 809.4 %reduce-scatter.25.cloned.1.call-start = ((), (), s32[]{:S(2)}) async-start(), calls=%async_computation.23 | async-start | bytes 16384000
  1740.4 3.9 copy-start
  1777.8 396.8 %reduce-scatter.21.cloned.1.call-start = ((), (), s32[]{:S(2)}) async-start(), calls=%async_computation.21 | async-start | bytes 16384000 | tf_op jit(solution)/shard_map/reduce_scatter | solution.py:46
  1799.1 477.4 %reduce-scatter.23.cloned.1.call-start = ((), (), s32[]{:S(2)}) async-start(), calls=%async_computation.22 | async-start | bytes 16384000 | tf_op jit(solution)/shard_map/reduce_scatter | solution.py:44
  1993.2 385.0 %reduce-scatter.19.cloned.1.call-start = ((), (), s32[]{:S(2)}) async-start(), calls=%async_computation.20 | async-start | bytes 16384000 | tf_op jit(solution)/shard_map/reduce_scatter | solution.py:44
  2015.1 487.2 %reduce-scatter.17.cloned.1.call-start = ((), (), s32[]{:S(2)}) async-start(), calls=%async_computation.19 | async-start | bytes 15728640 | tf_op jit(solution)/shard_map/reduce_scatter | solution.py:41
  2034.7 932.8 %all-reduce.3.cloned.1.call-start = ((), (), s32[]{:S(2)}) async-start(), calls=%async_computation.24 | async-start | bytes 27525120 | tf_op jit(solution)/shard_map/psum | solution.py:46
  2967.4 13.1 copy-start.1
Sparse Core Ops, SparseCore 0:
  9.5 71.7 all-gather.8
  82.9 47.8 all-gather.10
  132.4 47.8 all-gather.14
  181.7 247.7 all-gather.12
  430.9 47.8 all-gather.22
  480.2 47.8 all-gather.18
  530.3 68.9 all-gather.16
  601.6 458.8 reduce-scatter.10
  1113.0 121.8 reduce-scatter.12
  1262.7 458.8 reduce-scatter.14
  1723.2 247.7 all-gather.20
  1973.4 99.2 reduce-scatter.24
  2075.3 99.2 reduce-scatter.20
  2177.1 99.2 reduce-scatter.22
  2278.9 99.2 reduce-scatter.18
  2380.4 121.8 reduce-scatter.16
  2505.0 462.3 all-reduce.2
where the time goes:
time: 3000 us; the launch traced here: 2990 us
  waiting for transfers between devices  2630 us (88%)
  matrix products  275 us (9%)
  local copies, waits for them, and re-layouts  37.7 us (1%)
    reduce_scatter x2, waiting for transfers between devices, block_backward(): lax.psum_scatter(hidden_part, 'col', scatter_dimension=1, tiled=True)  919 us
    psum x1, waiting for transfers between devices, block_backward(): lax.psum(lax.psum_scatter(up_part, 'row', scatter_dimension=0, tiled=True...  461 us
    all_gather x2, waiting for transfers between devices, block_forward(): hidden_full = lax.all_gather(hidden, 'col', axis=1, tiled=True)  421 us
    reduce_scatter x2, waiting for transfers between devices, block_backward(): lax.psum_scatter(input_part, 'col', scatter_dimension=1, tiled=True)  223 us
    reduce_scatter x2, waiting for transfers between devices, block_backward(): lax.psum_scatter(down_part, 'row', scatter_dimension=0, tiled=True)  204 us
    all_gather x2, waiting for transfers between devices, block_forward(): acts_full = lax.all_gather(block_in, 'col', axis=1, tiled=True)  143 us
    reduce_scatter x1, waiting for transfers between devices, block_backward(): lax.psum_scatter(up_part, 'row', scatter_dimension=0, tiled=True)  96.8 us
    dot_general x4, matrix products, dot_last(): lax.dot_general(left_op, right_op, (((1,), (1,)), ((), ())), preferred_el...  84.9 us
  transfers between devices with their start and end apart: 17, of which 17 were waited for; matrix products, arithmetic and copies ran while one was open for 8% of the time, Pallas kernels for 0%

commit v1 on v0

v1 whole, which is shorter than its diff:
```python
import functools

import jax
import jax.numpy as jnp
from jax import lax
from jax.experimental import pallas as pl
from jax.experimental.pallas import tpu as pltpu
from jax.sharding import PartitionSpec as P

BF = jnp.bfloat16
F32 = jnp.float32
ROOT_2_PI = 0.7978845608028654
ANY = pl.BlockSpec(memory_space=pl.ANY)


class Place:
    def __init__(self):
        self.z = lax.axis_index("dep")
        self.y = lax.axis_index("col")
        row = lax.axis_index("row")
        self.x = row // 2
        self.k = row % 2
        self.half = self.z % 2

    def device(self, z=None, y=None, x=None, k=None):
        z = self.z if z is None else z
        y = self.y if y is None else y
        x = self.x if x is None else x
        k = self.k if k is None else k
        return {"dep": z, "col": y, "row": 2 * x + k}


def remote(src, dst, send_sem, recv_sem, device):
    return pltpu.make_async_remote_copy(
        src_ref=src, dst_ref=dst, send_sem=send_sem, recv_sem=recv_sem,
        device_id=device, device_id_type=pl.DeviceIdType.MESH)


def dot(left, right):
    return lax.dot_general(left, right, (((1,), (0,)), ((), ())), preferred_element_type=F32)


def dot_last(left, right):
    return lax.dot_general(left, right, (((1,), (1,)), ((), ())), preferred_element_type=F32)


def dot_first(left, right):
    return lax.dot_general(left, right, (((0,), (0,)), ((), ())), preferred_element_type=F32)


def gelu_pair(pre_act):
    tanh = jnp.tanh(ROOT_2_PI * (pre_act + 0.044715 * pre_act * pre_act * pre_act))
    half = 0.5 * (1.0 + tanh)
    slope = half + 0.5 * pre_act * (1.0 - tanh * tanh) * ROOT_2_PI * (1.0 + 3 * 0.044715 * pre_act * pre_act)
    return (pre_act * half).astype(BF), slope


PIECES = [(0, 0, 0), (0, 0, 1), (1, 0, 0), (0, 1, 0), (1, 1, 0), (1, 0, 1), (0, 1, 1), (1, 1, 1)]
N_SEM = 16


def gather_kernel(tok, grad, wu1, wd1, wu2, wd2, tok_full, grad_full, up1, down1, up2, down2,
                  stage_up, stage_down, stage_act, send, recv, local):
    here = Place()

    class Weight:
        def __init__(self, index, own, full):
            self.index, self.own, self.full = index, own, full
            self.rows, self.cols = own.shape

        def slot(self, dx, dy, other, twin=0):
            x = here.x if dx == 0 else 1 - here.x
            y = here.y if dy == 0 else 1 - here.y
            k = here.k if twin == 0 else 1 - here.k
            h = here.half if other == 0 else 1 - here.half
            half_rows = self.rows // 2
            start = pl.multiple_of((2 * x + k) * self.rows + h * half_rows, half_rows)
            return self.full.at[pl.ds(start, half_rows), pl.ds(pl.multiple_of(y * self.cols, self.cols), self.cols)]

        def own_half(self, other):
            h = here.half if other == 0 else 1 - here.half
            half_rows = self.rows // 2
            return self.own.at[pl.ds(pl.multiple_of(h * half_rows, half_rows), half_rows), :]

        def source(self, piece):
            return self.own_half(piece[2]) if piece[:2] == (0, 0) else self.slot(*piece)

        def hop(self, sem, piece, way):
            dx, dy, other = piece
            device = {"x": here.device(x=1 - here.x), "y": here.device(y=1 - here.y), "z": here.device(z=here.z + 1 - 2 * here.half),
                      "core": here.device(k=1 - here.k)}[way]
            arrived = {"x": (1 - dx, dy, other), "y": (dx, 1 - dy, other), "z": (dx, dy, 1 - other), "core": piece}[way]
            copy = remote(self.source(piece), self.slot(*piece), send.at[self.index, sem], recv.at[self.index, sem], device)
            copy.start()
            landed = self.slot(*arrived, twin=1 if way == "core" else 0)
            arrival = remote(landed, landed, send.at[self.index, sem], recv.at[self.index, sem], device)
            return copy, arrival

    weights = [Weight(i, own, full) for i, (own, full) in enumerate(((wu1, up1), (wd1, down1), (wu2, up2), (wd2, down2)))]
    sent = []
    arriving = {}

    def hop(m, piece, way):
        sem = {"x": 0, "y": 1, "z": 2, "core": 3}[way]
        key = (m, piece, way)
        number = len([1 for other in arriving if other[0] == m])
        copy, arrival = weights[m].hop(number, piece, way)
        sent.append(copy)
        arriving[key] = arrival

    def land(m, piece, way):
        arriving[(m, piece, way)].wait_recv()

    def act_copy(src, full, index):
        cols = src.shape[1]
        mine = full.at[:, pl.ds(pl.multiple_of(here.y * cols, cols), cols)]
        copy = remote(src, mine, send.at[4, index], recv.at[4, index], here.device(y=1 - here.y))
        copy.start()
        sent.append(copy)
        return copy

    def stage_in(src, buf, index):
        pltpu.make_async_copy(src, buf, local.at[index]).start()

    stages = [(wu1, stage_up.at[0], up1), (wd1, stage_down.at[0], down1), (wu2, stage_up.at[1], up2), (wd2, stage_down.at[1], down2)]

    def open_weight(m):
        hop(m, (0, 0, 0), "x")
        hop(m, (0, 0, 0), "y")
        hop(m, (0, 0, 0), "core")
        hop(m, (0, 0, 1), "core")

    def second(m):
        land(m, (0, 0, 0), "y")
        hop(m, (0, 1, 0), "x")
        hop(m, (0, 1, 0), "z")
        hop(m, (0, 1, 0), "core")
        land(m, (0, 0, 0), "x")
        hop(m, (1, 0, 0), "z")
        hop(m, (1, 0, 0), "core")

    def third(m):
        land(m, (0, 1, 0), "x")
        hop(m, (1, 1, 0), "z")
        hop(m, (1, 1, 0), "core")
        land(m, (0, 1, 0), "z")
        hop(m, (0, 1, 1), "core")
        land(m, (1, 0, 0), "z")
        hop(m, (1, 0, 1), "core")

    def fourth(m):
        land(m, (1, 1, 0), "z")
        hop(m, (1, 1, 1), "core")
        for piece in PIECES:
            land(m, piece, "core")

    open_weight(0)
    tok_copy = act_copy(tok, tok_full, 0)
    for i, (src, buf, full) in enumerate(stages):
        stage_in(src, buf, i)
    for i, src in enumerate((tok, grad)):
        stage_in(src, stage_act.at[i], 4 + i)
    outs = []
    for i, (src, buf, full) in enumerate(stages):
        pltpu.make_async_copy(src, buf, local.at[i]).wait()
        rows, cols = src.shape
        place = full.at[pl.ds(pl.multiple_of((2 * here.x + here.k) * rows, rows), rows), pl.ds(pl.multiple_of(here.y * cols, cols), cols)]
        outs.append(pltpu.make_async_copy(buf, place, local.at[i]))
        outs[-1].start()
    for i, (src, full) in enumerate(((tok, tok_full), (grad, grad_full))):
        pltpu.make_async_copy(src, stage_act.at[i], local.at[4 + i]).wait()
        cols = src.shape[1]
        place = full.at[:, pl.ds(pl.multiple_of(here.y * cols, cols), cols)]
        outs.append(pltpu.make_async_copy(stage_act.at[i], place, local.at[4 + i]))
        outs[-1].start()
    for m in range(4):
        second(m)
        if m < 3:
            open_weight(m + 1)
        if m == 2:
            grad_copy = act_copy(grad, grad_full, 1)
        third(m)
        if m > 0:
            fourth(m - 1)
    fourth(3)

    def landed_act(src, full, index):
        cols = src.shape[1]
        other = full.at[:, pl.ds(pl.multiple_of((1 - here.y) * cols, cols), cols)]
        remote(other, other, send.at[4, index], recv.at[4, index], here.device(y=1 - here.y)).wait_recv()

    landed_act(tok, tok_full, 0)
    landed_act(grad, grad_full, 1)
    for copy in sent:
        copy.wait_send()
    for copy in outs:
        copy.wait()


def gather_all(tok, wu1, wd1, wu2, wd2, grad):
    t, h = tok.shape
    r1, c1 = wu1.shape
    r2, c2 = wd1.shape
    shape = jax.ShapeDtypeStruct
    return pl.pallas_call(
        gather_kernel,
        out_shape=(shape((t, 2 * h), BF), shape((t, 2 * h), BF), shape((4 * r1, 2 * c1), BF), shape((4 * r2, 2 * c2), BF),
                   shape((4 * r1, 2 * c1), BF), shape((4 * r2, 2 * c2), BF)),
        in_specs=[ANY] * 6,
        out_specs=(ANY,) * 6,
        scratch_shapes=[pltpu.VMEM((2, r1, c1), BF), pltpu.VMEM((2, r2, c2), BF), pltpu.VMEM((2, t, h), BF),
                        pltpu.SemaphoreType.DMA((5, N_SEM)), pltpu.SemaphoreType.DMA((5, N_SEM)), pltpu.SemaphoreType.DMA((6,))],
        compiler_params=pltpu.CompilerParams(has_side_effects=True, vmem_limit_bytes=40 * 1024 * 1024),
        name="gather_all",
    )(tok, grad, wu1, wd1, wu2, wd2)


CHUNKS = 4


def reduce_kernel(*refs):
    parts, refs = refs[:4], refs[4:]
    outs, refs = refs[:4], refs[4:]
    from_twin, refs = refs[:4], refs[4:]
    to_x, from_x, mid, from_in, tot, from_ex = [refs[4 * i:4 * i + 4] for i in range(6)]
    refs = refs[24:]
    buf_up, buf_down, send, recv, lsem = refs
    here = Place()
    z_end = (here.z == 0) | (here.z == 3)
    inner = jnp.where(here.z == 0, 1, jnp.where(here.z == 3, 2, 3 - here.z))
    outer = jnp.where(here.z < 2, 0, 3)
    n_chunks = 4 * CHUNKS

    def chunk(ref, c, quarter=None):
        rows = ref.shape[0] // 4 if quarter is not None else ref.shape[0]
        step = rows // CHUNKS
        base = c * step if quarter is None else quarter * rows + c * step
        return ref.at[pl.ds(pl.multiple_of(base, step), step), :]

    def add(dst, *srcs):
        buf = buf_up if srcs[0].shape[1] > 1024 else buf_down
        copies = [pltpu.make_async_copy(src, buf.at[i], lsem.at[i]) for i, src in enumerate(srcs)]
        for copy in copies:
            copy.start()
        for copy in copies:
            copy.wait()
        total = buf[0]
        for i in range(1, len(srcs)):
            total = total + buf[i]
        buf[3] = total
        out = pltpu.make_async_copy(buf.at[3], dst, lsem.at[3])
        out.start()
        out.wait()

    def pair(src, dst, sem, i, device):
        return remote(src, dst, send.at[sem, i], recv.at[sem, i], device)

    def core_copy(i, which):
        m, c = divmod(i, CHUNKS)
        x = 1 - here.x if which == 0 else here.x
        rows = parts[m].shape[0] // 4
        src = chunk(parts[m], c, 2 * x + 1 - here.k)
        dst = from_twin[m].at[which, pl.ds(c * (rows // CHUNKS), rows // CHUNKS), :]
        return pair(src, dst, which, i, here.device(k=1 - here.k))

    def x_copy(i):
        m, c = divmod(i, CHUNKS)
        return pair(chunk(to_x[m], c), chunk(from_x[m], c), 2, i, here.device(x=1 - here.x))

    def in_copy(i):
        m, c = divmod(i, CHUNKS)
        return pair(chunk(mid[m], c), chunk(from_in[m], c), 3, i, here.device(z=inner))

    def ex_copy(i):
        m, c = divmod(i, CHUNKS)
        return pair(chunk(tot[m], c), chunk(from_ex[m], c), 4, i, here.device(z=inner))

    def out_copy(i):
        m, c = divmod(i, CHUNKS)
        return pair(chunk(outs[m], c), chunk(outs[m], c), 5, i, here.device(z=outer))

    def stage_core(i):
        core_copy(i, 0).start()
        core_copy(i, 1).start()

    def stage_x(i):
        m, c = divmod(i, CHUNKS)
        core_copy(i, 0).wait_recv()
        rows = parts[m].shape[0] // 4
        twin = from_twin[m].at[0, pl.ds(c * (rows // CHUNKS), rows // CHUNKS), :]
        add(chunk(to_x[m], c), chunk(parts[m], c, 2 * (1 - here.x) + here.k), twin)
        x_copy(i).start()

    def stage_mid(i):
        m, c = divmod(i, CHUNKS)
        core_copy(i, 1).wait_recv()
        x_copy(i).wait_recv()
        rows = parts[m].shape[0] // 4
        twin = from_twin[m].at[1, pl.ds(c * (rows // CHUNKS), rows // CHUNKS), :]
        add(chunk(mid[m], c), chunk(parts[m], c, 2 * here.x + here.k), twin, chunk(from_x[m], c))

        @pl.when(z_end)
        def _():
            in_copy(i).start()

    def stage_in(i):
        m, c = divmod(i, CHUNKS)

        @pl.when(~z_end)
        def _():
            in_copy(i).wait_recv()
            add(chunk(tot[m], c), chunk(mid[m], c), chunk(from_in[m], c))
            ex_copy(i).start()

    def stage_ex(i):
        m, c = divmod(i, CHUNKS)

        @pl.when(~z_end)
        def _():
            ex_copy(i).wait_recv()
            add(chunk(outs[m], c), chunk(tot[m], c), chunk(from_ex[m], c))
            out_copy(i).start()

    def stage_out(i):
        @pl.when(z_end)
        def _():
            out_copy(i).wait_recv()
            in_copy(i).wait_send()

        @pl.when(~z_end)
        def _():
            ex_copy(i).wait_send()
            out_copy(i).wait_send()

        core_copy(i, 0).wait_send()
        core_copy(i, 1).wait_send()
        x_copy(i).wait_send()

    stages = [stage_core, stage_x, stage_mid, stage_in, stage_ex, stage_out]
    for step in range(n_chunks + len(stages) - 1):
        for s, stage in enumerate(stages):
            if 0 <= step - s < n_chunks:
                stage(step - s)


def reduce_grads(parts):
    shape = jax.ShapeDtypeStruct
    quarters = [(p.shape[0] // 4, p.shape[1]) for p in parts]
    scratch_out = [shape((2,) + q, F32) for q in quarters] + [shape(q, F32) for _ in range(6) for q in quarters]
    up = max(quarters, key=lambda q: q[1])
    down = min(quarters, key=lambda q: q[1])
    n = 4 * CHUNKS
    results = pl.pallas_call(
        reduce_kernel,
        out_shape=tuple([shape(q, F32) for q in quarters] + scratch_out),
        in_specs=[ANY] * 4,
        out_specs=(ANY,) * (4 + len(scratch_out)),
        scratch_shapes=[pltpu.VMEM((4, up[0] // CHUNKS, up[1]), F32), pltpu.VMEM((4, down[0] // CHUNKS, down[1]), F32),
                        pltpu.SemaphoreType.DMA((6, n)), pltpu.SemaphoreType.DMA((6, n)), pltpu.SemaphoreType.DMA((4,))],
        compiler_params=pltpu.CompilerParams(has_side_effects=True, vmem_limit_bytes=40 * 1024 * 1024),
        name="reduce_grads",
    )(*parts)
    return results[:4]


def solution(mesh):
    act_spec = P(("dep", "row"), "col")
    weight_spec = P("row", "col")

    def local_step(tokens, w_up1, w_down1, w_up2, w_down2, grad_out):
        y = lax.axis_index("col")

        def my_cols(arr):
            width = arr.shape[1] // 2
            return lax.dynamic_slice(arr, (0, y * width), (arr.shape[0], width))

        def my_rows(arr):
            height = arr.shape[0] // 2
            return lax.dynamic_slice(arr, (y * height, 0), (height, arr.shape[1]))

        x_full, g_full, up1, down1, up2, down2 = gather_all(tokens, w_up1, w_down1, w_up2, w_down2, grad_out)
        hid1, slope1 = gelu_pair(dot(x_full, up1))
        mid = (x_full.astype(F32) + dot(hid1, down1)).astype(BF)
        hid2, slope2 = gelu_pair(dot(mid, up2))
        part_down2 = dot_first(hid2, grad_out)
        y_out = (my_cols(mid).astype(F32) + dot(hid2, my_cols(down2))).astype(BF)
        dpre2 = (dot_last(g_full, down2) * slope2).astype(BF)
        part_up2 = dot_first(mid, my_cols(dpre2))
        dmid = (g_full.astype(F32) + dot_last(dpre2, up2)).astype(BF)
        part_down1 = dot_first(hid1, my_cols(dmid))
        dpre1 = (dot_last(dmid, down1) * slope1).astype(BF)
        part_up1 = dot_first(x_full, my_cols(dpre1))
        grad_x = (my_cols(dmid).astype(F32) + dot_last(dpre1, my_rows(up1))).astype(BF)
        grad_down2, grad_up2, grad_down1, grad_up1 = reduce_grads([part_down2, part_up2, part_down1, part_up1])
        return y_out, grad_x, grad_up1, grad_down1, grad_up2, grad_down2

    return jax.shard_map(local_step, mesh=mesh, in_specs=(act_spec, weight_spec, weight_spec, weight_spec, weight_spec, act_spec), out_specs=(act_spec, act_spec, weight_spec, weight_spec, weight_spec, weight_spec), check_vma=False)
```

time: 3000 us -> 1060 us (0.35)
  waiting for transfers between devices: 2630 us -> 0 us
  Pallas kernels: 0 us -> 623 us
  matrix products: 275 us -> 409 us
    reduce_scatter x7 -> x0, waiting for transfers between devices: 1440 us -> none  [the longest x2 919 us: block_backward(): lax.psum_scatter(hidden_part, 'col', scatter_dimension=1, tiled=True)]
    all_gather x8 -> x0, waiting for transfers between devices: 687 us -> none  [the longest x2 421 us: block_forward(): hidden_full = lax.all_gather(hidden, 'col', axis=1, tiled=True)]
    pallas_call x0 -> x2, Pallas kernels: none -> 623 us  [the longest x1 358 us: reduce_grads(): pl.pallas_call(reduce_kernel, out_shape=tuple([shape(q, F32) for q in qua...]
    psum x1 -> x0, waiting for transfers between devices: 461 us -> none  [block_backward(): lax.psum(lax.psum_scatter(up_part, 'row', scatter_dimension=0, tiled=True...]
    dot_general x12, matrix products: 275 us -> 409 us  [the longest x4 172 us: dot_last(): lax.dot_general(left, right, (((1,), (1,)), ((), ())), preferred_element_...]
    unnamed x18 -> x0, waiting for transfers between devices: 42 us -> none
  transfers between devices with their start and end apart: 17 -> 0, of which waited for: 17 -> 0; matrix products, arithmetic and copies ran while one was open for 8% -> 0% of each run, Pallas kernels for 0% -> 0%
where the time goes in v1:
time: 1060 us; the launch traced here: 1050 us
  Pallas kernels  623 us (59%)
  matrix products  409 us (39%)
  local copies, waits for them, and re-layouts  16.1 us (2%)
    pallas_call x1, Pallas kernels, reduce_grads(): pl.pallas_call(reduce_kernel, out_shape=tuple([shape(q, F32) for q in qua...  358 us
    pallas_call x1, Pallas kernels, gather_all(): pl.pallas_call(gather_kernel, out_shape=(shape((t, 2 * h), BF), shape((t,...  265 us
    dot_general x4, matrix products, dot_last(): lax.dot_general(left, right, (((1,), (1,)), ((), ())), preferred_element_...  172 us
    dot_general x4, matrix products, dot(): lax.dot_general(left, right, (((1,), (0,)), ((), ())), preferred_element_...  147 us
    dot_general x4, matrix products, dot_first(): lax.dot_general(left, right, (((0,), (0,)), ((), ())), preferred_element_...  89.8 us

profile of v1, /device:TPU:0, one launch (start us, length us, event | category | flops | bytes accessed | tf_op | source)
XLA Modules:
  0.0 1048.7 jit_solution(5664565778565047227)
XLA Ops:
  0.6 0.0 copy-start
  0.7 1.7 copy-done
  2.4 1.7 copy-done.1
  4.1 1.4 copy-done.3
  5.6 1.4 copy-done.4
  7.0 1.4 copy-done.5
  8.4 1.4 copy-done.6
  9.8 264.7 %gather_all.1 = (bf16[2048,1280]{1,0:T(8,128)(2,1)}, bf16[2048,1280]{1,0:T(8,128)(2,1)}, bf16[1280,5120]{1,0:T(8,128)(2,1)}, bf16[5120,1280]{1,0:T(8,128)(2,1)},...) custom-call(bf16[2048,640]{1,0:T(8,128)(2,1)S(1)} %copy-done, bf16[2048,640]{1,0:T(8,128)(2,1)S(1)} %copy-done.1, ...), custom_call_target="tpu_custom_call" | custom-call | tf_op jit(solution)/shard_map/gather_all/pallas_call | solution.py:205
  274.5 0.0 copy-start.8
  274.5 34.9 %fusion.33 = f32[2048,5120]{1,0:T(8,128)} fusion(bf16[2048,1280]{1,0:T(8,128)(2,1)} %get-tuple-element.16, bf16[1280,5120]{1,0:T(8,128)(2,1)} %get-tuple-element.17), kind=kOutput, calls=%fused_computation.41 | convolution fusion | flops 26843545600 | bytes 60293120 | tf_op jit(solution)/shard_map/dot_general | solution.py:40
  309.5 0.0 copy-done.8
  309.5 44.6 %add_convert_fusion.1 = bf16[2048,1280]{1,0:T(8,128)(2,1)} fusion(bf16[2048,1280]{1,0:T(8,128)(2,1)S(1)} %copy-done.8, bf16[5120,1280]{1,0:T(8,128)(2,1)} %get-tuple-element.18, f32[2048,5120]{1,0:T(8,128)} %fusion.33), kind=kOutput, calls=%fused_computation.27 | convolution fusion | flops 26945781760 | bytes 65536000 | tf_op jit(solution)/shard_map/dot_general | solution.py:40
  354.1 44.8 %multiply_convert_fusion = (bf16[2048,5120]{1,0:T(8,128)(2,1)}, f32[2048,5120]{1,0:T(8,128)}) fusion(bf16[2048,1280]{1,0:T(8,128)(2,1)} %add_convert_fusion.1, bf16[1280,5120]{1,0:T(8,128)(2,1)} %get-tuple-element.19), kind=kOutput, calls=%fused_computation.18 | convolution fusion | flops 26937917440 | bytes 81264640 | tf_op jit(solution)/shard_map/dot_general | solution.py:40
  398.9 0.0 copy-done.10
  398.9 57.5 %fusion.8 = bf16[2048,5120]{1,0:T(8,128)(2,1)} fusion(f32[2048,5120]{1,0:T(8,128)} %get-tuple-element.27, bf16[2048,1280]{1,0:T(8,128)(2,1)S(1)} %copy-done.10, bf16[5120,1280]{1,0:T(8,128)(2,1)} %get-tuple-element.20), kind=kOutput, calls=%fused_computation.12 | convolution fusion | flops 27042775040 | bytes 81264640 | tf_op jit(solution)/shard_map/dot_general | solution.py:44
  456.4 36.1 %add_convert_fusion = bf16[2048,1280]{1,0:T(8,128)(2,1)} fusion(bf16[2048,1280]{1,0:T(8,128)(2,1)} %get-tuple-element.21, bf16[2048,5120]{1,0:T(8,128)(2,1)} %fusion.8, bf16[1280,5120]{1,0:T(8,128)(2,1)} %get-tuple-element.19), kind=kOutput, calls=%fused_computation.26 | convolution fusion | flops 26851409920 | bytes 44564480 | tf_op jit(solution)/shard_map/dot_general | solution.py:44
  492.4 22.6 %add_convert_fusion.3 = bf16[2048,640]{1,0:T(8,128)(2,1)} fusion(bf16[2048,5120]{1,0:T(8,128)(2,1)} %get-tuple-element.26, bf16[5120,1280]{1,0:T(8,128)(2,1)} %get-tuple-element.20, s32[]{:T(128)S(6)} %select_n.4, bf16[2048,1280]{1,0:T(8,128)(2,1)} %add_convert_fusion.1), kind=kOutput, calls=%fused_computation.33 | convolution fusion | flops 13425704960 | bytes 32769024 | tf_op jit(solution)/shard_map/dot_general | solution.py:40
  515.0 0.0 copy-done.11
  515.0 20.0 %fusion.16.refs_1_ = f32[1280,2560]{1,0:T(8,128)} fusion(bf16[2048,1280]{1,0:T(8,128)(2,1)S(1)} %copy-done.11, bf16[2048,5120]{1,0:T(8,128)(2,1)} %fusion.8, s32[]{:T(128)S(6)} %select_n.5), kind=kOutput, calls=%fused_computation.24 | convolution fusion | flops 13421772800 | bytes 28835844 | tf_op jit(solution)/shard_map/dot_general | solution.py:48
  535.1 0.0 copy-done.2
  535.1 21.6 %fusion.34.refs_0_ = f32[5120,640]{1,0:T(8,128)} fusion(bf16[2048,5120]{1,0:T(8,128)(2,1)} %get-tuple-element.26, bf16[2048,640]{1,0:T(8,128)(2,1)S(1)} %copy-done.2), kind=kOutput, calls=%fused_computation.42 | convolution fusion | flops 13421772800 | bytes 36700160 | tf_op jit(solution)/shard_map/dot_general | solution.py:48
  556.7 0.0 slice-done
  556.7 0.0 slice-done.1
  556.7 57.6 %fusion.13 = bf16[2048,5120]{1,0:T(8,128)(2,1)} fusion(f32[2048,5120]{1,0:T(8,128)} %fusion.33, bf16[2048,1280]{1,0:T(8,128)(2,1)S(1)} %bitcast.18, bf16[5120,1280]{1,0:T(8,128)(2,1)} %get-tuple-element.18), kind=kOutput, calls=%fused_computation.17 | convolution fusion | flops 27042775040 | bytes 81264640 | tf_op jit(solution)/shard_map/dot_general | solution.py:44
  614.3 28.3 %fusion.26.refs_2_ = f32[5120,640]{1,0:T(8,128)} fusion(bf16[2048,1280]{1,0:T(8,128)(2,1)S(1)} %bitcast.18, s32[]{:T(128)S(6)} %select_n.4, f32[2048,5120]{1,0:T(8,128)} %fusion.33), kind=kOutput, calls=%fused_computation.34 | convolution fusion | flops 13516144640 | bytes 57671684 | tf_op jit(solution)/shard_map/dot_general | solution.py:48
  642.6 20.9 %add_convert_fusion.2 = bf16[2048,640]{1,0:T(8,128)(2,1)} fusion(bf16[2048,5120]{1,0:T(8,128)(2,1)} %fusion.13, bf16[1280,5120]{1,0:T(8,128)(2,1)S(1)} %copy-done.7, s32[]{:T(128)S(6)} %select_n.4, bf16[2048,1280]{1,0:T(8,128)(2,1)} %add_convert_fusion), kind=kOutput, calls=%fused_computation.32 | convolution fusion | flops 13425704960 | bytes 32769024 | tf_op jit(solution)/shard_map/dot_general | solution.py:44
  663.5 19.9 %fusion.14.refs_3_ = f32[1280,2560]{1,0:T(8,128)} fusion(bf16[2048,1280]{1,0:T(8,128)(2,1)S(1)} %copy-done.9, bf16[2048,5120]{1,0:T(8,128)(2,1)} %fusion.13, s32[]{:T(128)S(6)} %select_n.5), kind=kOutput, calls=%fused_computation.22 | convolution fusion | flops 13421772800 | bytes 28835844 | tf_op jit(solution)/shard_map/dot_general | solution.py:48
  683.3 358.3 %reduce_grads.1 = (f32[1280,640]{1,0:T(8,128)S(1)}, f32[320,2560]{1,0:T(8,128)S(1)}, f32[1280,640]{1,0:T(8,128)S(1)}, f32[320,2560]{1,0:T(8,128)S(1)}, f32[2,128...) custom-call(f32[5120,640]{1,0:T(8,128)} %fusion.34.refs_0_, ...), custom_call_target="tpu_custom_call" | custom-call | tf_op jit(solution)/shard_map/reduce_grads/pallas_call | solution.py:353
  1041.7 1.7 copy.16
  1043.4 1.7 copy.17
  1045.1 1.7 copy.18
  1046.8 1.7 copy.19
  (15 shorter events, 0.0 us)
Async XLA Ops:
  0.6 1.7 copy-start
  2.4 1.7 copy-start.1
  4.1 1.4 copy-start.3
  5.6 1.4 copy-start.4
  7.0 1.4 copy-start.5
  8.4 1.4 copy-start.6
  274.5 35.0 %copy-start.8 = (bf16[2048,1280]{1,0:T(8,128)(2,1)S(1)}, bf16[2048,1280]{1,0:T(8,128)(2,1)}, u32[]{:S(2)}) copy-start(bf16[2048,1280]{1,0:T(8,128)(2,1)} %get-tuple-element.16) | copy-start | bytes 15728644
  354.1 44.8 %copy-start.10 = (bf16[2048,1280]{1,0:T(8,128)(2,1)S(1)}, bf16[2048,1280]{1,0:T(8,128)(2,1)}, u32[]{:S(2)}) copy-start(bf16[2048,1280]{1,0:T(8,128)(2,1)} %get-tuple-element.21) | copy-start | bytes 15728644
  492.4 22.6 %copy-start.11 = (bf16[2048,1280]{1,0:T(8,128)(2,1)S(1)}, bf16[2048,1280]{1,0:T(8,128)(2,1)}, u32[]{:S(2)}) copy-start(bf16[2048,1280]{1,0:T(8,128)(2,1)} %add_convert_fusion.1) | copy-start | bytes 15728644
  515.0 20.1 %copy-start.2 = (bf16[2048,640]{1,0:T(8,128)(2,1)S(1)}, bf16[2048,640]{1,0:T(8,128)(2,1)}, u32[]{:S(2)}) copy-start(bf16[2048,640]{1,0:T(8,128)(2,1)} %grad.1) | copy-start | bytes 7864324
  515.0 41.7 %slice-start = ((s8[5242880]{0:T(1024)(128)(4,1)}), s8[4194304]{0:T(1024)(128)(4,1)S(1)}, s32[]{:S(2)}) async-start(s8[5242880]{0:T(1024)(128)(4,1)} %bitcast.17), calls=%async_computation | async-start | bytes 8388608
  535.1 21.6 %slice-start.1 = ((s8[5242880]{0:T(1024)(128)(4,1)}), s8[1048576]{0:T(1024)(128)(4,1)S(1)}, s32[]{:S(2)}) async-start(s8[5242880]{0:T(1024)(128)(4,1)} %bitcast.17), calls=%async_computation.1 | async-start | bytes 2097152
  614.3 28.3 %copy-start.7 = (bf16[1280,5120]{1,0:T(8,128)(2,1)S(1)}, bf16[1280,5120]{1,0:T(8,128)(2,1)}, u32[]{:S(2)}) copy-start(bf16[1280,5120]{1,0:T(8,128)(2,1)} %get-tuple-element.17) | copy-start | bytes 39321604
  642.6 20.9 %copy-start.9 = (bf16[2048,1280]{1,0:T(8,128)(2,1)S(1)}, bf16[2048,1280]{1,0:T(8,128)(2,1)}, u32[]{:S(2)}) copy-start(bf16[2048,1280]{1,0:T(8,128)(2,1)} %get-tuple-element.16) | copy-start | bytes 15728644

commit v2 on v0

v2 whole, which is shorter than its diff:
```python
import functools

import jax
import jax.numpy as jnp
from jax import lax
from jax.experimental import pallas as pl
from jax.experimental.pallas import tpu as pltpu
from jax.sharding import PartitionSpec as P

BF = jnp.bfloat16
F32 = jnp.float32
ROOT_2_PI = 0.7978845608028654
CUBIC = 0.044715
ANY = pl.BlockSpec(memory_space=pl.ANY)


class Place:
    def __init__(self):
        self.z = lax.axis_index("dep")
        self.y = lax.axis_index("col")
        row = lax.axis_index("row")
        self.x = row // 2
        self.k = row % 2
        self.half = self.z % 2

    def device(self, z=None, y=None, x=None, k=None):
        z = self.z if z is None else z
        y = self.y if y is None else y
        x = self.x if x is None else x
        k = self.k if k is None else k
        return {"dep": z, "col": y, "row": 2 * x + k}


def remote(src, dst, send_sem, recv_sem, device):
    return pltpu.make_async_remote_copy(
        src_ref=src, dst_ref=dst, send_sem=send_sem, recv_sem=recv_sem,
        device_id=device, device_id_type=pl.DeviceIdType.MESH)


def dot(left, right):
    return lax.dot_general(left, right, (((1,), (0,)), ((), ())), preferred_element_type=F32)


def dot_last(left, right):
    return lax.dot_general(left, right, (((1,), (1,)), ((), ())), preferred_element_type=F32)


def dot_first(left, right):
    return lax.dot_general(left, right, (((0,), (0,)), ((), ())), preferred_element_type=F32)


def gelu_pair(pre_act):
    square = pre_act * pre_act
    half = 0.5 + 0.5 * jnp.tanh(pre_act * (ROOT_2_PI + (ROOT_2_PI * CUBIC) * square))
    slope = half + ((half - half * half) * pre_act) * (2 * ROOT_2_PI + (6 * CUBIC * ROOT_2_PI) * square)
    return (pre_act * half).astype(BF), slope


CONTRACT = {"nn": (((1,), (0,)), ((), ())), "nt": (((1,), (1,)), ((), ())), "tn": (((0,), (0,)), ((), ()))}


def matmul(left, right, outs, form, tile, epilogue, extra=(), rows_inner=True, hooks=()):
    depth = left.shape[0] if form == "tn" else left.shape[1]
    rows = left.shape[1] if form == "tn" else left.shape[0]
    cols = right.shape[0] if form == "nt" else right.shape[1]
    tm, tn = tile
    grid = (cols // tn, rows // tm) if rows_inner else (rows // tm, cols // tn)
    assert all(at < grid[0] * grid[1] for at, _ in hooks)

    def spec(shape, index):
        return pl.BlockSpec(shape, (lambda n, m: index(m, n)) if rows_inner else index)

    left_spec = spec((depth, tm), lambda m, n: (0, m)) if form == "tn" else spec((tm, depth), lambda m, n: (m, 0))
    right_spec = spec((tn, depth), lambda m, n: (n, 0)) if form == "nt" else spec((depth, tn), lambda m, n: (0, n))
    tile_spec = spec((tm, tn), lambda m, n: (m, n))

    def body(left_ref, right_ref, *rest):
        step = pl.program_id(0) * grid[1] + pl.program_id(1)
        for at, action in hooks:
            pl.when(step == at)(action)
        product = lax.dot_general(left_ref[...], right_ref[...], CONTRACT[form], preferred_element_type=F32)
        results = epilogue(product, *[ref[...] for ref in rest[:len(extra)]])
        for ref, value in zip(rest[len(extra):], results):
            ref[...] = value

    pltpu.emit_pipeline(body, grid=grid, in_specs=[left_spec, right_spec] + [tile_spec] * len(extra),
                        out_specs=[tile_spec] * len(outs))(left, right, *extra, *outs)


def plain(product):
    return (product,)


def residual(product, base):
    return ((base.astype(F32) + product).astype(BF),)


def halves(ref, y):
    width = ref.shape[1] // 2
    return [ref.at[:, pl.ds(pl.multiple_of(h * width, width), width)] for h in (y, 1 - y)]


def tokens_of(ref, part, parts):
    step = ref.shape[0] // parts
    return ref.at[pl.ds(part * step, step), :]


OWN = (0, 0, 0)
OWN_ALL = (0, 0, 2)
X_NEAR = (1, 0, 0)
X_REST = (1, 0, 1)
X_ALL = (1, 0, 2)
Y_NEAR = (0, 1, 0)
Y_REST = (0, 1, 1)
DIAG_NEAR = (1, 1, 0)
DIAG_REST = (1, 1, 1)
UP1, DOWN1, UP2, DOWN2 = range(4)

N_SEM = 16
ACT_PARTS = 4


def forward_kernel(tok, grad, wu1, wd1, wu2, wd2, tok_full, grad_full, up1, down1, up2, down2,
                   hid1, slope1, mid, hid2, slope2, part_down2,
                   stage_up, stage_down, stage_act, send, recv, act_send, act_recv, local):
    here = Place()

    class Weight:
        def __init__(self, index, own, full):
            self.index, self.own, self.full = index, own, full
            self.rows, self.cols = own.shape

        def slot(self, dx, dy, other, twin=0):
            x = here.x if dx == 0 else 1 - here.x
            y = here.y if dy == 0 else 1 - here.y
            k = here.k if twin == 0 else 1 - here.k
            h = 0 if other == 2 else here.half if other == 0 else 1 - here.half
            height = self.rows if other == 2 else self.rows // 2
            start = pl.multiple_of((2 * x + k) * self.rows + h * height, height)
            return self.full.at[pl.ds(start, height), pl.ds(pl.multiple_of(y * self.cols, self.cols), self.cols)]

        def source(self, piece):
            if piece[:2] != (0, 0):
                return self.slot(*piece)
            if piece[2] == 2:
                return self.own
            h = here.half if piece[2] == 0 else 1 - here.half
            height = self.rows // 2
            return self.own.at[pl.ds(pl.multiple_of(h * height, height), height), :]

    weights = [Weight(i, own, full) for i, (own, full) in enumerate(((wu1, up1), (wd1, down1), (wu2, up2), (wd2, down2)))]
    slots = {}
    landed = set()

    def number(m, piece, way):
        return slots.setdefault((m, piece, way), len([key for key in slots if key[0] == m]))

    def neighbour(way):
        return {"x": here.device(x=1 - here.x), "y": here.device(y=1 - here.y), "z": here.device(z=here.z + 1 - 2 * here.half),
                "core": here.device(k=1 - here.k)}[way]

    def beyond(piece, way):
        dx, dy, other = piece
        return {"x": (1 - dx, dy, other), "y": (dx, 1 - dy, other), "z": (dx, dy, 1 - other if other < 2 else 2), "core": piece}[way]

    def hop(m, piece, way, start=True):
        n = number(m, piece, way)
        copy = remote(weights[m].source(piece), weights[m].slot(*piece), send.at[m, n], recv.at[m, n], neighbour(way))
        if start:
            copy.start()
        else:
            copy.wait_send()

    def land(m, way, piece):
        n = number(m, beyond(piece, way), way)
        landed.add((m, beyond(piece, way), way))
        place = weights[m].slot(*piece, twin=1 if way == "core" else 0)
        remote(place, place, send.at[m, n], recv.at[m, n], neighbour(way)).wait_recv()

    def act_copy(src, full, index, part, wait=None):
        cols, height = src.shape[1], src.shape[0] // ACT_PARTS
        rows = pl.ds(part * height, height)

        def place(y):
            return full.at[rows, pl.ds(pl.multiple_of(y * cols, cols), cols)]

        sems = act_send.at[index, part], act_recv.at[index, part]
        if wait == "recv":
            remote(place(1 - here.y), place(1 - here.y), *sems, neighbour("y")).wait_recv()
            return
        copy = remote(src.at[rows, :], place(here.y), *sems, neighbour("y"))
        if wait == "send":
            copy.wait_send()
        else:
            copy.start()

    def land_all(m):
        for key in [key for key in slots if key[0] == m and key[2] == "core" and key not in landed]:
            land(m, "core", key[1])

    hop(UP1, OWN, "x")
    hop(UP1, OWN, "y")
    hop(UP1, OWN_ALL, "core")
    for part in range(ACT_PARTS):
        if part == ACT_PARTS - 1:
            hop(DOWN1, OWN, "y")
        act_copy(tok, tok_full, 0, part)
    for m in (UP2, DOWN2):
        hop(m, OWN, "y")
    for part in range(ACT_PARTS):
        act_copy(grad, grad_full, 1, part)

    stages = [(wu1, stage_up.at[0], up1), (wd1, stage_down.at[0], down1), (wu2, stage_up.at[1], up2), (wd2, stage_down.at[1], down2)]
    own_places = []
    for src, buf, full in stages:
        rows, cols = src.shape
        own_places.append((src, buf, full.at[pl.ds(pl.multiple_of((2 * here.x + here.k) * rows, rows), rows),
                                             pl.ds(pl.multiple_of(here.y * cols, cols), cols)]))
    for i, (src, full) in enumerate(((tok, tok_full), (grad, grad_full))):
        cols = src.shape[1]
        own_places.append((src, stage_act.at[i], full.at[:, pl.ds(pl.multiple_of(here.y * cols, cols), cols)]))
    for i, (src, buf, place) in enumerate(own_places):
        pltpu.make_async_copy(src, buf, local.at[i]).start()
    outs = []
    for i, (src, buf, place) in enumerate(own_places):
        pltpu.make_async_copy(src, buf, local.at[i]).wait()
        outs.append(pltpu.make_async_copy(buf, place, local.at[i]))
        outs[-1].start()
    for copy in outs:
        copy.wait()

    def pass_on(m, way, piece, *ways):
        def action():
            land(m, way, piece)
            for onward in ways:
                hop(m, piece, onward)
            hop(m, piece, "core")
        return action

    def begin(*sends):
        def action():
            for m, piece, way in sends:
                hop(m, piece, way)
        return action

    def run(*actions):
        for action in actions:
            action()

    def up(act, weight, hid, slope, hooks=()):
        rows = act.shape[0]
        matmul(act, weight, (hid, slope), "nn", (rows, 512 if rows < 2048 else 256), gelu_pair, hooks=hooks)

    up1_h, hid1_h, slope1_h = [halves(ref, here.y) for ref in (up1, hid1, slope1)]
    up2_h, hid2_h, slope2_h = [halves(ref, here.y) for ref in (up2, hid2, slope2)]

    def up_part(h, first, count, hooks=()):
        height = tok.shape[0] // ACT_PARTS
        rows = pl.ds(first * height, count * height)
        up(tok_full.at[rows, :], up1_h[h], hid1_h[h].at[rows, :], slope1_h[h].at[rows, :], hooks)

    def tokens_land(*parts):
        for part in parts:
            act_copy(tok, tok_full, 0, part, "recv")

    def near_core(m):
        for piece in (OWN_ALL, X_NEAR, X_REST):
            land(m, "core", piece)

    run(pass_on(UP1, "x", X_NEAR, "z"), pass_on(UP1, "y", Y_NEAR, "x", "z"),
        begin((DOWN1, OWN, "x"), (DOWN1, OWN_ALL, "core"), (UP2, OWN_ALL, "core"), (DOWN2, OWN_ALL, "core")),
        pass_on(UP1, "z", X_REST), pass_on(UP1, "x", DIAG_NEAR, "z"))
    near_core(UP1)
    tokens_land(0, 1)
    up_part(0, 0, 2, [(3, pass_on(UP1, "z", Y_REST)), (4, pass_on(DOWN1, "x", X_NEAR))])
    tokens_land(2)
    up_part(0, 2, 1)
    run(pass_on(UP1, "z", DIAG_REST))
    land_all(UP1)
    up_part(1, 0, 2, [(3, pass_on(DOWN1, "y", Y_NEAR, "x", "z")), (3, begin((DOWN1, X_NEAR, "z")))])
    up_part(1, 2, 1)
    run(pass_on(DOWN1, "x", DIAG_NEAR), pass_on(DOWN1, "z", Y_REST, "x"), begin((UP2, OWN, "x")))
    tokens_land(3)
    up_part(0, 3, 1)
    up_part(1, 3, 1, [(2, pass_on(UP2, "y", Y_NEAR, "z", "x"))])
    run(pass_on(DOWN1, "z", X_REST), pass_on(DOWN1, "x", DIAG_REST))
    land_all(DOWN1)
    matmul(hid1, down1, (mid,), "nn", (1024, 256), residual, extra=(tok_full,), rows_inner=False,
           hooks=[(3, pass_on(UP2, "z", Y_REST, "x")), (5, pass_on(UP2, "x", X_NEAR, "z")), (5, pass_on(DOWN2, "y", Y_NEAR, "z")),
                  (5, begin((DOWN2, OWN, "x"), (DOWN2, Y_NEAR, "x"))), (9, pass_on(UP2, "x", DIAG_NEAR))])
    run(pass_on(UP2, "z", X_REST))
    near_core(UP2)
    up(mid, up2_h[0], hid2_h[0], slope2_h[0], [(7, pass_on(UP2, "x", DIAG_REST)), (8, pass_on(DOWN2, "z", Y_REST, "x"))])
    land_all(UP2)
    up(mid, up2_h[1], hid2_h[1], slope2_h[1], [(4, pass_on(DOWN2, "x", X_NEAR, "z"))])
    matmul(hid2, grad, (part_down2,), "tn", (1280, 640), plain, rows_inner=False,
           hooks=[(0, pass_on(DOWN2, "x", DIAG_NEAR)), (1, pass_on(DOWN2, "z", X_REST)), (3, pass_on(DOWN2, "x", DIAG_REST))])
    for m in (DOWN2, DOWN1, UP1):
        land_all(m)
    for part in range(ACT_PARTS):
        act_copy(grad, grad_full, 1, part, "recv")
    assert landed == set(slots)
    for m, piece, way in slots:
        hop(m, piece, way, start=False)
    for part in range(ACT_PARTS):
        act_copy(tok, tok_full, 0, part, "send")
        act_copy(grad, grad_full, 1, part, "send")


def forward(tok, wu1, wd1, wu2, wd2, grad):
    t, h = tok.shape
    r1, c1 = wu1.shape
    r2, c2 = wd1.shape
    ffn = 2 * c1
    shape = jax.ShapeDtypeStruct
    return pl.pallas_call(
        forward_kernel,
        out_shape=(shape((t, 2 * h), BF), shape((t, 2 * h), BF), shape((4 * r1, 2 * c1), BF), shape((4 * r2, 2 * c2), BF),
                   shape((4 * r1, 2 * c1), BF), shape((4 * r2, 2 * c2), BF),
                   shape((t, ffn), BF), shape((t, ffn), F32), shape((t, 2 * h), BF), shape((t, ffn), BF), shape((t, ffn), F32),
                   shape((ffn, h), F32)),
        in_specs=[ANY] * 6,
        out_specs=(ANY,) * 12,
        scratch_shapes=[pltpu.VMEM((2, r1, c1), BF), pltpu.VMEM((2, r2, c2), BF), pltpu.VMEM((2, t, h), BF),
                        pltpu.SemaphoreType.DMA((4, N_SEM)), pltpu.SemaphoreType.DMA((4, N_SEM)),
                        pltpu.SemaphoreType.DMA((2, ACT_PARTS)), pltpu.SemaphoreType.DMA((2, ACT_PARTS)), pltpu.SemaphoreType.DMA((6,))],
        compiler_params=pltpu.CompilerParams(has_side_effects=True, vmem_limit_bytes=60 * 1024 * 1024),
        name="forward",
    )(tok, grad, wu1, wd1, wu2, wd2)


CHUNKS = 8
SLOTS = 4
PERIOD = 8.7


def backward_kernel(*refs):
    (grad, grad_full, tok_full, mid, hid1, hid2, slope1, slope2, up1, down1, up2, down2, part_down2), refs = refs[:13], refs[13:]
    (y_out, grad_x, *outs), refs = refs[:6], refs[6:]
    (dpre2, dmid, dpre1, part_up2, part_down1, part_up1), refs = refs[:6], refs[6:]
    from_twin, from_x, from_in, from_ex = [refs[4 * i:4 * i + 4] for i in range(4)]
    buf_up, buf_down, send, recv, load_sem, store_sem = refs[16:]
    parts = [part_down2, part_up2, part_down1, part_up1]
    here = Place()
    z_end = (here.z == 0) | (here.z == 3)
    inner = jnp.where(here.z == 0, 1, jnp.where(here.z == 3, 2, 3 - here.z))
    outer = jnp.where(here.z < 2, 0, 3)
    total = 4 * CHUNKS
    LOAD, XS, MID, TOT, OUT = 0, 7, 7 + SLOTS, 7 + 2 * SLOTS, 7 + 3 * SLOTS

    def rows_of(i, quarter=None):
        height = parts[i // CHUNKS].shape[0] // 4
        step = height // CHUNKS
        base = (i % CHUNKS) * step
        return pl.ds(base if quarter is None else pl.multiple_of(quarter * height + base, step), step)

    def buf(i, index):
        return (buf_up if parts[i // CHUNKS].shape[1] > 1024 else buf_down).at[index]

    def slot(i, first):
        return buf(i, first + i % SLOTS)

    def part(i, quarter):
        return parts[i // CHUNKS].at[rows_of(i, quarter), :]

    def row_block(ref, i):
        return ref[i // CHUNKS].at[rows_of(i), :]

    def twin(i, which):
        return from_twin[i // CHUNKS].at[which, rows_of(i), :]

    def copy(kind, src, dst, i, device):
        return remote(src, dst, send.at[kind, i], recv.at[kind, i], device)

    def core_copy(i, which):
        x = 1 - here.x if which == 0 else here.x
        return copy(which, part(i, 2 * x + 1 - here.k), twin(i, which), i, here.device(k=1 - here.k))

    def x_copy(i):
        return copy(2, slot(i, XS), row_block(from_x, i), i, here.device(x=1 - here.x))

    def in_copy(i):
        return copy(3, slot(i, MID), row_block(from_in, i), i, here.device(z=inner))

    def ex_copy(i):
        return copy(4, slot(i, TOT), row_block(from_ex, i), i, here.device(z=inner))

    def out_copy(i):
        return copy(5, slot(i, OUT), row_block(outs, i), i, here.device(z=outer))

    def store(i):
        return pltpu.make_async_copy(slot(i, OUT), row_block(outs, i), store_sem.at[i % SLOTS])

    def load(i, index, src):
        return pltpu.make_async_copy(src, buf(i, LOAD + index), load_sem.at[index])

    def add(dst, *srcs):
        height, width = dst.shape
        step = 8 if width > 1024 else 16

        @pl.loop(0, height // step)
        def _(j):
            rows = pl.ds(pl.multiple_of(j * step, step), step)
            value = srcs[0][rows, :]
            for src in srcs[1:]:
                value = value + src[rows, :]
            dst[rows, :] = value

    def start_core(i):
        core_copy(i, 0).start()
        core_copy(i, 1).start()

    def x_loads(i):
        return [load(i, 0, part(i, 2 * (1 - here.x) + here.k)), load(i, 1, twin(i, 0))]

    def mid_loads(i):
        return [load(i, 2, part(i, 2 * here.x + here.k)), load(i, 3, twin(i, 1)), load(i, 4, row_block(from_x, i))]

    def even(j):
        def action():
            cm, ci, ce = j - 2, j - 4, j - 6
            if j + 1 < total:
                start_core(j + 1)
            if j < total:
                for c in x_loads(j):
                    c.wait()
                if j >= SLOTS:
                    x_copy(j - SLOTS).wait_send()
                add(slot(j, XS), buf(j, 0), buf(j, 1))
                x_copy(j).start()
            if 0 <= cm < total:
                for c in mid_loads(cm):
                    c.wait()
                if cm >= SLOTS:
                    @pl.when(z_end)
                    def _():
                        in_copy(cm - SLOTS).wait_send()
                add(slot(cm, MID), buf(cm, 2), buf(cm, 3), buf(cm, 4))

            @pl.when(z_end)
            def _():
                if 0 <= cm < total:
                    in_copy(cm).start()

            @pl.when(~z_end)
            def _():
                if 0 <= ce < total:
                    load(ce, 6, row_block(from_ex, ce)).wait()
                    if ce >= SLOTS:
                        out_copy(ce - SLOTS).wait_send()
                        store(ce - SLOTS).wait()
                    add(slot(ce, OUT), slot(ce, TOT), buf(ce, 6))
                    store(ce).start()
                    out_copy(ce).start()
                if 0 <= ci < total:
                    load(ci, 5, row_block(from_in, ci)).wait()
                    if ci >= SLOTS:
                        ex_copy(ci - SLOTS).wait_send()
                    add(slot(ci, TOT), slot(ci, MID), buf(ci, 5))
                    ex_copy(ci).start()
        return action

    def odd(j):
        def action():
            cx, cm, ci, ce = j + 1, j - 1, j - 3, j - 5
            if cx < total:
                core_copy(cx, 0).wait_recv()
                for c in x_loads(cx):
                    c.start()
            if 0 <= cm < total:
                core_copy(cm, 1).wait_recv()
                x_copy(cm).wait_recv()
                for c in mid_loads(cm):
                    c.start()

            @pl.when(~z_end)
            def _():
                if 0 <= ci < total:
                    in_copy(ci).wait_recv()
                    load(ci, 5, row_block(from_in, ci)).start()
                if 0 <= ce < total:
                    ex_copy(ce).wait_recv()
                    load(ce, 6, row_block(from_ex, ce)).start()
        return action

    actions = [(0.0, 0, odd(-1))]
    for j in range(total + 6):
        actions.append((j * PERIOD + 1.0, min(j + 1, total - 1) // CHUNKS, even(j)))
        actions.append(((j + 0.5) * PERIOD + 1.0, min(j + 1, total - 1) // CHUNKS, odd(j)))

    def my(ref, axis):
        size = ref.shape[axis] // 2
        place = pl.ds(pl.multiple_of(here.y * size, size), size)
        return ref.at[:, place] if axis == 1 else ref.at[place, :]

    def scaled(product, slope):
        return ((product * slope).astype(BF),)

    dpre2_h, slope2_h = halves(dpre2, here.y), halves(slope2, here.y)
    dpre1_h, slope1_h = halves(dpre1, here.y), halves(slope1, here.y)

    def row_halves(ref):
        height = ref.shape[0] // 2
        return [ref.at[pl.ds(pl.multiple_of(h * height, height), height), :] for h in (here.y, 1 - here.y)]

    down2_h, down1_h = row_halves(down2), row_halves(down1)
    dmid_h = halves(dmid, here.y)

    def pre(left, h, down_h, dpre_h, slope_h):
        return lambda hooks: matmul(left, down_h[h], (dpre_h[h],), "nt", (2048, 256), scaled, extra=(slope_h[h],), hooks=hooks)

    def into_mid(hooks):
        matmul(dpre2, up2, (dmid,), "nt", (1024, 256), residual, extra=(grad_full,), rows_inner=False, hooks=hooks)

    tasks = [
        (10, 24, 0, pre(grad_full, 0, down2_h, dpre2_h, slope2_h)),
        (5, 22.5, 1, lambda hooks: matmul(mid, dpre2_h[0], (part_up2,), "tn", (1280, 512), plain, hooks=hooks)),
        (10, 24, 1, pre(grad_full, 1, down2_h, dpre2_h, slope2_h)),
        (10, 37, 1, into_mid),
        (8, 23.5, 2, lambda hooks: matmul(hid1, dmid_h[0], (part_down1,), "tn", (640, 640), plain, rows_inner=False, hooks=hooks)),
        (10, 24, 2, pre(dmid, 0, down1_h, dpre1_h, slope1_h)),
        (5, 22.5, 3, lambda hooks: matmul(tok_full, dpre1_h[0], (part_up1,), "tn", (1280, 512), plain, hooks=hooks)),
        (10, 24, 3, pre(dmid, 1, down1_h, dpre1_h, slope1_h)),
        (8, 24, 3, lambda hooks: matmul(hid2, my(down2, 1), (y_out,), "nn", (256, 640), residual, extra=(my(mid, 1),), hooks=hooks)),
        (8, 24, 3, lambda hooks: matmul(dpre1, my(up1, 0), (grad_x,), "nt", (256, 640), residual, extra=(my(dmid, 1),), hooks=hooks)),
    ]
    start_core(0)
    clock, ready, position = 0.0, 0, 0
    for steps, length, after, call in tasks:
        hooks = []
        for step in range(steps):
            while position < len(actions) and actions[position][0] <= clock and actions[position][1] <= ready:
                hooks.append((step, actions[position][2]))
                position += 1
                clock += 0.6
            clock += length / steps
        call(hooks)
        ready = after
    for _, _, action in actions[position:]:
        action()

    for i in range(total):
        core_copy(i, 0).wait_send()
        core_copy(i, 1).wait_send()
    for i in range(total - SLOTS, total):
        x_copy(i).wait_send()

    @pl.when(z_end)
    def _():
        for i in range(total):
            out_copy(i).wait_recv()
        for i in range(total - SLOTS, total):
            in_copy(i).wait_send()

    @pl.when(~z_end)
    def _():
        for i in range(total - SLOTS, total):
            ex_copy(i).wait_send()
            out_copy(i).wait_send()
            store(i).wait()


def backward(grad, grad_full, tok_full, mid, hid1, hid2, slope1, slope2, up1, down1, up2, down2, part_down2):
    shape = jax.ShapeDtypeStruct
    t, h = grad.shape
    ffn = hid1.shape[1]
    up_part, down_part = (2 * h, ffn // 2), part_down2.shape
    order = [down_part, up_part, down_part, up_part]
    quarters = [(p[0] // 4, p[1]) for p in order]
    outs = [shape((t, h), BF)] * 2 + [shape(q, F32) for q in quarters]
    work = [shape((t, ffn), BF), shape((t, 2 * h), BF), shape((t, ffn), BF), shape(up_part, F32), shape(down_part, F32), shape(up_part, F32)]
    landing = [shape((2,) + q, F32) for q in quarters] + [shape(q, F32) for _ in range(3) for q in quarters]
    n = 4 * CHUNKS
    depth = 7 + 4 * SLOTS
    args = (grad, grad_full, tok_full, mid, hid1, hid2, slope1, slope2, up1, down1, up2, down2, part_down2)
    results = pl.pallas_call(
        backward_kernel,
        out_shape=tuple(outs + work + landing),
        in_specs=[ANY] * len(args),
        out_specs=(ANY,) * (len(outs) + len(work) + len(landing)),
        scratch_shapes=[pltpu.VMEM((depth, quarters[1][0] // CHUNKS, quarters[1][1]), F32), pltpu.VMEM((depth, quarters[0][0] // CHUNKS, quarters[0][1]), F32),
                        pltpu.SemaphoreType.DMA((6, n)), pltpu.SemaphoreType.DMA((6, n)), pltpu.SemaphoreType.DMA((7,)), pltpu.SemaphoreType.DMA((SLOTS,))],
        compiler_params=pltpu.CompilerParams(has_side_effects=True, vmem_limit_bytes=62 * 1024 * 1024),
        name="backward",
    )(*args)
    return results[:6]


def solution(mesh):
    act_spec = P(("dep", "row"), "col")
    weight_spec = P("row", "col")

    def local_step(tokens, w_up1, w_down1, w_up2, w_down2, grad_out):
        (x_full, g_full, up1, down1, up2, down2, hid1, slope1, mid, hid2, slope2, part_down2) = forward(
            tokens, w_up1, w_down1, w_up2, w_down2, grad_out)
        y_out, grad_x, grad_down2, grad_up2, grad_down1, grad_up1 = backward(
            grad_out, g_full, x_full, mid, hid1, hid2, slope1, slope2, up1, down1, up2, down2, part_down2)
        return y_out, grad_x, grad_up1, grad_down1, grad_up2, grad_down2

    return jax.shard_map(local_step, mesh=mesh, in_specs=(act_spec, weight_spec, weight_spec, weight_spec, weight_spec, act_spec), out_specs=(act_spec, act_spec, weight_spec, weight_spec, weight_spec, weight_spec), check_vma=False)
```

time: 3000 us -> 674 us (0.22)
  waiting for transfers between devices: 2630 us -> 0 us
  Pallas kernels: 0 us -> 650 us
  matrix products: 275 us -> 0 us
    reduce_scatter x7 -> x0, waiting for transfers between devices: 1440 us -> none  [the longest x2 919 us: block_backward(): lax.psum_scatter(hidden_part, 'col', scatter_dimension=1, tiled=True)]
    all_gather x8 -> x0, waiting for transfers between devices: 687 us -> none  [the longest x2 421 us: block_forward(): hidden_full = lax.all_gather(hidden, 'col', axis=1, tiled=True)]
    pallas_call x0 -> x2, Pallas kernels: none -> 650 us  [the longest x1 374 us: backward(): pl.pallas_call(backward_kernel, out_shape=tuple(outs + work + landing), i...]
    psum x1 -> x0, waiting for transfers between devices: 461 us -> none  [block_backward(): lax.psum(lax.psum_scatter(up_part, 'row', scatter_dimension=0, tiled=True...]
    dot_general x12 -> x0, matrix products: 275 us -> none  [the longest x4 84.9 us: dot_last(): lax.dot_general(left_op, right_op, (((1,), (1,)), ((), ())), preferred_el...]
    unnamed x18 -> x0, waiting for transfers between devices: 42 us -> none
  transfers between devices with their start and end apart: 17 -> 0, of which waited for: 17 -> 0; matrix products, arithmetic and copies ran while one was open for 8% -> 0% of each run, Pallas kernels for 0% -> 0%
where the time goes in v2:
time: 674 us; the launch traced here: 668 us
  Pallas kernels  650 us (96%)
  local copies, waits for them, and re-layouts  17.5 us (3%)
    pallas_call x1, Pallas kernels, backward(): pl.pallas_call(backward_kernel, out_shape=tuple(outs + work + landing), i...  374 us
    pallas_call x1, Pallas kernels, forward(): pl.pallas_call(forward_kernel, out_shape=(shape((t, 2 * h), BF), shape((t...  276 us
    unnamed x16, local copies, waits for them, and re-layouts  17.5 us

profile of v2, /device:TPU:0, one launch (start us, length us, event | category | flops | bytes accessed | tf_op | source)
XLA Modules:
  0.0 668.3 jit_solution(1556112362020962144)
XLA Ops:
  0.6 275.6 %forward.1 = (bf16[2048,1280]{1,0:T(8,128)(2,1)}, bf16[2048,1280]{1,0:T(8,128)(2,1)}, bf16[1280,5120]{1,0:T(8,128)(2,1)}, bf16[5120,1280]{1,0:T(8,128)(2,1)}, bf...) custom-call(bf16[2048,640]{1,0:T(8,128)(2,1)} %tok.1, ...), custom_call_target="tpu_custom_call" | custom-call | tf_op jit(solution)/shard_map/forward/pallas_call | solution.py:316
  276.3 374.1 %backward.1 = (bf16[2048,640]{1,0:T(8,128)(2,1)}, bf16[2048,640]{1,0:T(8,128)(2,1)}, f32[1280,640]{1,0:T(8,128)}, f32[320,2560]{1,0:T(8,128)}, f32[1280,640]{1,0...) custom-call(bf16[2048,640]{1,0:T(8,128)(2,1)} %refs_0_.1, ...), custom_call_target="tpu_custom_call" | custom-call | tf_op jit(solution)/shard_map/backward/pallas_call | solution.py:576
  650.4 0.0 copy-start.4
  650.4 3.6 copy.18
  654.0 0.0 copy-done.4
  654.0 0.0 copy-start.3
  654.0 1.5 copy.19
  655.5 1.4 copy-done.3
  656.9 0.0 copy-start.2
  656.9 1.7 copy.20
  658.6 1.4 copy-done.2
  660.0 0.0 copy-start.1
  660.0 1.7 copy.21
  661.7 1.4 copy-done.1
  663.1 0.0 copy-start
  663.1 1.7 copy.22
  664.8 1.4 copy-done
  666.2 1.7 copy.23
Async XLA Ops:
  650.4 3.6 copy-start.4
  654.0 2.9 copy-start.3
  656.9 3.1 copy-start.2
  660.0 3.1 copy-start.1
  663.1 3.1 copy-start

commit v3 on v2

--- a/solution.py
+++ b/solution.py
@@ -252,7 +252,6 @@
         matmul(act, weight, (hid, slope), "nn", (rows, 512 if rows < 2048 else 256), gelu_pair, hooks=hooks)
 
     up1_h, hid1_h, slope1_h = [halves(ref, here.y) for ref in (up1, hid1, slope1)]
-    up2_h, hid2_h, slope2_h = [halves(ref, here.y) for ref in (up2, hid2, slope2)]
 
     def up_part(h, first, count, hooks=()):
         height = tok.shape[0] // ACT_PARTS
@@ -290,11 +289,28 @@
                   (5, begin((DOWN2, OWN, "x"), (DOWN2, Y_NEAR, "x"))), (9, pass_on(UP2, "x", DIAG_NEAR))])
     run(pass_on(UP2, "z", X_REST))
     near_core(UP2)
-    up(mid, up2_h[0], hid2_h[0], slope2_h[0], [(7, pass_on(UP2, "x", DIAG_REST)), (8, pass_on(DOWN2, "z", Y_REST, "x"))])
-    land_all(UP2)
-    up(mid, up2_h[1], hid2_h[1], slope2_h[1], [(4, pass_on(DOWN2, "x", X_NEAR, "z"))])
-    matmul(hid2, grad, (part_down2,), "tn", (1280, 640), plain, rows_inner=False,
-           hooks=[(0, pass_on(DOWN2, "x", DIAG_NEAR)), (1, pass_on(DOWN2, "z", X_REST)), (3, pass_on(DOWN2, "x", DIAG_REST))])
+    half_width = up2.shape[1] // 2
+
+    @pl.loop(0, 2)
+    def _(turn):
+        def rest():
+            for piece in (Y_NEAR, Y_REST, DIAG_NEAR, DIAG_REST):
+                land(UP2, "core", piece)
+
+        def at_turn(wanted, action):
+            def guarded():
+                pl.when(turn == wanted)(action)
+            return guarded
+
+        pl.when(turn == 1)(rest)
+        columns = pl.ds(pl.multiple_of((here.y + turn) % 2 * half_width, half_width), half_width)
+        up(mid, up2.at[:, columns], hid2.at[:, columns], slope2.at[:, columns],
+           [(7, at_turn(0, pass_on(UP2, "x", DIAG_REST))), (8, at_turn(0, pass_on(DOWN2, "z", Y_REST, "x"))),
+            (9, at_turn(1, pass_on(DOWN2, "x", X_NEAR, "z")))])
+
+    matmul(hid2, grad, (part_down2,), "tn", (640, 640), plain, rows_inner=False,
+           hooks=[(2, pass_on(DOWN2, "x", DIAG_NEAR)), (6, pass_on(DOWN2, "x", DIAG_REST))])
+    run(pass_on(DOWN2, "z", X_REST))
     for m in (DOWN2, DOWN1, UP1):
         land_all(m)
     for part in range(ACT_PARTS):
@@ -586,6 +602,30 @@
     return results[:6]
 
 
+def hand_over_kernel(*refs):
+    sources, results, buffers = refs[:6], refs[6:12], refs[12:18]
+    loads, stores = refs[18:]
+    for i, (src, buf) in enumerate(zip(sources, buffers)):
+        pltpu.make_async_copy(src, buf, loads.at[i]).start()
+    for i, (src, buf, dst) in enumerate(zip(sources, buffers, results)):
+        pltpu.make_async_copy(src, buf, loads.at[i]).wait()
+        pltpu.make_async_copy(buf, dst, stores.at[i]).start()
+    for i, (buf, dst) in enumerate(zip(buffers, results)):
+        pltpu.make_async_copy(buf, dst, stores.at[i]).wait()
+
+
+def hand_over(arrays):
+    return pl.pallas_call(
+        hand_over_kernel,
+        out_shape=tuple(jax.ShapeDtypeStruct(arr.shape, arr.dtype) for arr in arrays),
+        in_specs=[ANY] * 6,
+        out_specs=(ANY,) * 6,
+        scratch_shapes=[pltpu.VMEM(arr.shape, arr.dtype) for arr in arrays] + [pltpu.SemaphoreType.DMA((6,)), pltpu.SemaphoreType.DMA((6,))],
+        compiler_params=pltpu.CompilerParams(vmem_limit_bytes=60 * 1024 * 1024),
+        name="hand_over",
+    )(*arrays)
+
+
 def solution(mesh):
     act_spec = P(("dep", "row"), "col")
     weight_spec = P("row", "col")
@@ -595,6 +635,6 @@
             tokens, w_up1, w_down1, w_up2, w_down2, grad_out)
         y_out, grad_x, grad_down2, grad_up2, grad_down1, grad_up1 = backward(
             grad_out, g_full, x_full, mid, hid1, hid2, slope1, slope2, up1, down1, up2, down2, part_down2)
-        return y_out, grad_x, grad_up1, grad_down1, grad_up2, grad_down2
+        return hand_over((y_out, grad_x, grad_up1, grad_down1, grad_up2, grad_down2))
 
     return jax.shard_map(local_step, mesh=mesh, in_specs=(act_spec, weight_spec, weight_spec, weight_spec, weight_spec, act_spec), out_specs=(act_spec, act_spec, weight_spec, weight_spec, weight_spec, weight_spec), check_vma=False)

time: 674 us -> 657 us (0.975)
  local copies, waits for them, and re-layouts: 17.5 us -> 0 us
    unnamed x16 -> x0, local copies, waits for them, and re-layouts: 17.5 us -> none
    pallas_call x0 -> x1, Pallas kernels: none -> 12.5 us  [hand_over(): pl.pallas_call(hand_over_kernel, out_shape=tuple((jax.ShapeDtypeStruct(ar...]
    pallas_call x1, Pallas kernels: 276 us -> 269 us  [forward(): pl.pallas_call(forward_kernel, out_shape=(shape((t, 2 * h), BF), shape((t...]
where the time goes in v3:
time: 657 us; the launch traced here: 654 us
  Pallas kernels  653 us (99%)
    pallas_call x1, Pallas kernels, backward(): pl.pallas_call(backward_kernel, out_shape=tuple(outs + work + landing), i...  372 us
    pallas_call x1, Pallas kernels, forward(): pl.pallas_call(forward_kernel, out_shape=(shape((t, 2 * h), BF), shape((t...  269 us

profile of v3, /device:TPU:0, one launch (start us, length us, event | category | flops | bytes accessed | tf_op | source)
XLA Modules:
  0.0 654.0 jit_solution(11618041764986087593)
XLA Ops:
  0.6 268.5 %forward.1 = (bf16[2048,1280]{1,0:T(8,128)(2,1)}, bf16[2048,1280]{1,0:T(8,128)(2,1)}, bf16[1280,5120]{1,0:T(8,128)(2,1)}, bf16[5120,1280]{1,0:T(8,128)(2,1)}, bf...) custom-call(bf16[2048,640]{1,0:T(8,128)(2,1)} %tok.1, ...), custom_call_target="tpu_custom_call" | custom-call | tf_op jit(solution)/shard_map/forward/pallas_call | solution.py:332
  269.2 372.2 %backward.1 = (bf16[2048,640]{1,0:T(8,128)(2,1)}, bf16[2048,640]{1,0:T(8,128)(2,1)}, f32[1280,640]{1,0:T(8,128)}, f32[320,2560]{1,0:T(8,128)}, f32[1280,640]{1,0...) custom-call(bf16[2048,640]{1,0:T(8,128)(2,1)} %refs_0_.1, ...), custom_call_target="tpu_custom_call" | custom-call | tf_op jit(solution)/shard_map/backward/pallas_call | solution.py:592
  641.3 12.5 %hand_over.1 = (bf16[2048,640]{1,0:T(8,128)(2,1)}, bf16[2048,640]{1,0:T(8,128)(2,1)}, f32[320,2560]{1,0:T(8,128)}, f32[1280,640]{1,0:T(8,128)}, f32[320,2560]{1,0:T(8,128)}, /*index=5*/f32[1280,640]{1,0:T(8,128)}) custom-call(bf16[2048,640]{1,0:T(8,128)(2,1)} %get-tuple-element.36.refs_0_, bf16[2048,640]{1,0:T(8,128)(2,1)} %get-tuple-element.37.refs_1_, ...), custom_call_target="tpu_custom_call" | custom-call | tf_op jit(solution)/shard_map/hand_over/pallas_call | solution.py:618
